TPU v7x, 32 devices: a whole 2x2x4 slice. The times are simulated.
32 devices in a mesh: node: 8 (over z, y), feat: 4 (over x, core).
Axes of the slice: x: 2, y: 2, z: 4, core: 2. Of those that a mesh axis runs over, the one named last changes fastest.
Arguments:
- mesh_nodes: bfloat16 [2048, 512], P('node', 'feat'), may hold values from -6 to 6
- mesh_edges: bfloat16 [16384, 512], P(('node', 'feat')), may hold values from -6 to 6
- grid_nodes: bfloat16 [4096, 512], P('node', 'feat'), may hold values from -6 to 6
- m2g_edges: bfloat16 [12288, 512], P(('node', 'feat')), may hold values from -6 to 6
- edge_receivers: int32 [16384], P(('node', 'feat')), may hold values from 0 to 255
- edge_slots: int32 [16384], P(('node', 'feat')), may hold values from 0 to 1023
- send_rows: int32 [8, 8, 128], P('node'), may hold values from 0 to 255
- m2g_slots: int32 [12288], P(('node', 'feat')), may hold values from 0 to 1023
- m2g_send_rows: int32 [8, 8, 128], P('node'), may hold values from 0 to 255
- edge_w_in: bfloat16 [3, 3, 512, 512], replicated, may hold values from -0.15625 to 0.15625
- edge_w_out: bfloat16 [3, 512, 512], replicated, may hold values from -0.25 to 0.25
- edge_bias: float32 [3, 2, 512], replicated, may hold values from -2 to 2
- edge_gain: float32 [3, 512], replicated, may hold values from 0.5 to 1.5
- edge_shift: float32 [3, 512], replicated, may hold values from -2 to 2
- node_w_in: bfloat16 [3, 2, 512, 512], P(None, None, 'feat'), may hold values from -0.1875 to 0.1875
- node_w_out: bfloat16 [3, 512, 512], P(None, 'feat'), may hold values from -0.25 to 0.25
- node_bias: float32 [3, 2, 512], P(None, None, 'feat'), may hold values from -2 to 2
- node_gain: float32 [3, 512], P(None, 'feat'), may hold values from 0.5 to 1.5
- node_shift: float32 [3, 512], P(None, 'feat'), may hold values from -2 to 2
Outputs:
- grid_out: bfloat16 [4096, 512], P('node', 'feat')
All inputs are finite; a program needn't handle non-finite values.
Results may differ from a plain program's by a relative error of at most 0.015.
Values may be sent and summed in bfloat16 or wider, within the bound.
A program may use at most 64 MiB of HBM per device.

v0:
```python
import functools

import jax
import jax.numpy as jnp
from jax import lax
from jax.experimental import pallas as pl
from jax.experimental.pallas import tpu as pltpu
from jax.sharding import PartitionSpec as P

EPSILON = 1e-05
LANES = 128
BF16 = jnp.bfloat16
F32 = jnp.float32
MESH = pl.DeviceIdType.MESH


def dot(a, b):
    return jnp.dot(a, b, preferred_element_type=F32)


def at(start, size):
    return pl.ds(pl.multiple_of(start * size, size), size)


def column(row):
    return jnp.transpose(jnp.broadcast_to(row, (LANES, row.shape[1])))


def fill_picks(ref, row):
    col = column(row)
    lane = lax.broadcasted_iota(jnp.int32, col.shape, 1)
    for c in range(0, ref.shape[1], LANES):
        ref[:, c : c + LANES] = jnp.where(col == lane + c, 1.0, 0.0).astype(BF16)


def finish_mlp(pre, base, w_out, bias_out, gain, shift):
    hidden = (pre / (1.0 + jnp.exp(-pre))).astype(BF16)
    out = dot(hidden, w_out) + bias_out
    mean = jnp.mean(out, axis=-1, keepdims=True)
    variance = jnp.mean(out * out, axis=-1, keepdims=True) - mean * mean
    normed = (out - mean) * lax.rsqrt(variance + EPSILON) * gain + shift
    return (base.astype(F32) + normed).astype(BF16)


def kernel(n, feats, counts, *refs):
    (
        nodes, edges_hbm, grid_hbm, links_hbm, recv_row, slot_row, table_row, link_row, link_table_row,
        ew_in_hbm, ew_out_hbm, ebias, egain, eshift, nw_in_hbm, nw_out_hbm, nbias, ngain, nshift,
        out,
        edges, links, ew_in, ew_out, nw_in, nw_out, nb, ng, ns,
        pick_table, pick_link_table, pick_slot, pick_recv, sum_recv, pick_link, pick_cell, sum_cell,
        acc, part, chip_sum, rs_buf, cells, upd, wide, outgoing, extra, arrived,
        load_sem, send_sem, recv_sem,
    ) = refs
    sections = ew_in.shape[0]
    last = sections - 1
    p = lax.axis_index("node")
    f = lax.axis_index("feat")
    half = feats // 2
    chip = lax.div(f, 2)
    core = lax.rem(f, 2)
    partner = f + 1 - 2 * core
    role = lax.rem(p, 2)
    beside = p + 1 - 2 * role
    block_half = n // 2
    rows_all, share = nodes.shape
    own_rows = rows_all // 2
    cell_count = cells.shape[0]
    next_sem = [0]

    def sems(count):
        base = next_sem[0]
        next_sem[0] += count
        return base

    def remote(src, dst, sem, **where):
        return pltpu.make_async_remote_copy(
            src_ref=src, dst_ref=dst, send_sem=send_sem.at[sem], recv_sem=recv_sem.at[sem],
            device_id=where, device_id_type=MESH,
        )

    def node_at(k):
        return lax.rem(p + k, n)

    def node_from(k):
        return lax.rem(p + n - k, n)

    def feat_at(k):
        return lax.rem(f + k, feats)

    def chip_at(m):
        return lax.rem(chip + m, half) * 2 + core

    def chip_from(m):
        return lax.rem(chip + half - m, half) * 2 + core

    barrier = pltpu.get_barrier_semaphore()

    def greet(k, carry):
        pl.semaphore_signal(barrier, inc=1, device_id={"node": node_at(k)}, device_id_type=MESH)
        return carry

    lax.fori_loop(1, n, greet, 0)
    for k in range(1, feats):
        pl.semaphore_signal(barrier, inc=1, device_id={"feat": feat_at(k)}, device_id_type=MESH)

    loads = {}

    def load(name, src, dst):
        copy = pltpu.make_async_copy(src, dst, load_sem.at[len(loads)])
        copy.start()
        loads[name] = copy

    load("wide", nodes, wide.at[0, :, at(f, share)])
    load("edges", edges_hbm, edges)
    for t in range(sections):
        load(("ew_in", t), ew_in_hbm.at[t], ew_in.at[t])
        load(("ew_out", t), ew_out_hbm.at[t], ew_out.at[t])
        load(("nw_in", t), nw_in_hbm.at[t], nw_in.at[t, :, at(f, share), :])
        load(("nw_out", t), nw_out_hbm.at[t], nw_out.at[t, at(f, share), :])
    load("links", links_hbm, links)
    load("cells", grid_hbm.at[at(f, cell_count), :], cells.at[:, at(f, share)])
    load("nb", nbias, nb.at[f])
    load("ng", ngain, ng.at[f])
    load("ns", nshift, ns.at[f])

    pick_refs = [pick_table] * last + [pick_link_table]
    slots = [c // n for c in counts]

    fill_picks(pick_table, table_row[...])
    first_out = dot(pick_table[...], nodes[...]).astype(BF16)
    outgoing[0, : counts[0], :] = first_out

    pl.semaphore_wait(barrier, n - 1 + feats - 1)

    node_sem = [sems(n) for _ in range(sections)]
    near_sem = [sems(n) for _ in range(sections)]
    chips = range(1, half)
    far_sem = [{m: sems(n) for m in chips} for _ in range(sections)]
    relay_sem = [{m: sems(n) for m in chips} for _ in range(sections)]
    extra_sem = [{m: sems(n) for m in chips} for _ in range(sections)]

    def node_copy(t, k):
        dst = node_at(k)
        return remote(
            outgoing.at[t, at(dst, slots[t]), :],
            arrived.at[t, at(p, slots[t]), at(f, share)],
            node_sem[t] + k, node=dst,
        )

    def extra_copy(t, k, m):
        dst = node_at(k)
        return remote(
            extra.at[t, m, at(dst, slots[t]), :],
            arrived.at[t, at(p, slots[t]), at(chip_from(m), share)],
            extra_sem[t][m] + k, node=dst,
        )

    def if_close(other, yes, no):
        close = lax.div(other, block_half) == lax.div(p, block_half)
        if yes is not None:
            pl.when(close)(yes)
        if no is not None:
            pl.when(jnp.logical_not(close))(no)

    def block(t, k, who):
        return arrived.at[t, at(node_from(k), slots[t]), at(who, share)]

    def near_copy(t, k):
        return remote(block(t, k, f), block(t, k, f), near_sem[t] + k, feat=partner)

    def far_copy(t, k, m):
        return remote(block(t, k, f), block(t, k, f), far_sem[t][m] + k, feat=chip_at(m))

    def relay_copy(t, k, m):
        who = chip_from(m)
        return remote(block(t, k, who), block(t, k, who), relay_sem[t][m] + k, feat=partner)

    def each(fn, low=1, high=n):
        def body(k, carry):
            fn(k)
            return carry

        lax.fori_loop(low, high, body, 0)

    def spread(t):
        lag = 2

        def relay_now(k):
            for m in chips:
                far_copy(t, k, m).wait_recv()
                relay_copy(t, k, m).start()

        def far_start(k):
            for m in chips:
                far_copy(t, k, m).start()

        def extra_relay(k):
            for m in chips:
                extra_copy(t, k, m).wait_recv()
                relay_copy(t, k, m).start()

        def take(k):
            node_copy(t, k).wait_recv()
            near_copy(t, k).start()

        def step(k):
            take(k)
            far_start(k)

            @pl.when(k > lag)
            def _():
                relay_now(k - lag)

        def cross(k):
            take(k)
            far_start(k)

        def direct(k):
            take(k)
            extra_relay(k)

        if t == 0:
            each(step)
            each(relay_now, max(1, n - lag), n)
        else:
            each(lambda k: if_close(node_from(k), None, lambda: cross(k)))
            each(lambda k: if_close(node_from(k), lambda: direct(k), None))
            each(lambda k: if_close(node_from(k), None, lambda: relay_now(k)))

    def settle(t):
        def far_done(k):
            for m in chips:
                far_copy(t, k, m).wait_send()

        def extra_done(k):
            for m in chips:
                extra_copy(t, k, m).wait_send()

        def step(k):
            node_copy(t, k).wait_send()
            near_copy(t, k).wait()
            if t == 0:
                far_done(k)
            else:
                if_close(node_from(k), None, lambda: far_done(k))
                if_close(node_at(k), lambda: extra_done(k), None)
            for m in chips:
                relay_copy(t, k, m).wait()

        each(step)

    def extra_start(t, k):
        def go():
            for m in chips:
                extra_copy(t, k, m).start()

        if_close(node_at(k), go, None)

    def weight_copies(near_src, near_dst, half_src, half_dst):
        group = {"near": [remote(near_src, near_dst, sems(1), feat=partner)]}
        for name in ("far", "back", "side", "last"):
            group[name] = []
        for m in chips:
            who = chip_from(m)
            group["far"].append(remote(half_src, half_dst(f, role), sems(1), feat=chip_at(m)))
            group["back"].append(remote(half_dst(who, role), half_dst(who, role), sems(1), feat=partner))
            group["side"].append(remote(half_dst(who, role), half_dst(who, role), sems(1), node=beside))
            other = half_dst(who, 1 - role)
            group["last"].append(remote(other, other, sems(1), feat=partner))
        return group

    half_share = share // 2

    def out_rows(who, part_id):
        return at(who * 2 + part_id, half_share)

    weights_in = [
        weight_copies(
            nw_in_hbm.at[t], nw_in.at[t, :, at(f, share), :], nw_in_hbm.at[t, role],
            lambda who, part_id, t=t: nw_in.at[t, part_id, at(who, share), :],
        )
        for t in range(sections)
    ]
    weights_out = [
        weight_copies(
            nw_out_hbm.at[t], nw_out.at[t, at(f, share), :], nw_out_hbm.at[t, at(role, half_share), :],
            lambda who, part_id, t=t: nw_out.at[t, out_rows(who, part_id), :],
        )
        for t in range(sections)
    ]

    def begin(group):
        for copy in group["far"] + group["near"]:
            copy.start()

    def pass_on(group):
        for far, back, side in zip(group["far"], group["back"], group["side"]):
            far.wait_recv()
            side.start()
            back.start()

    def pass_last(group):
        for side, copy in zip(group["side"], group["last"]):
            side.wait_recv()
            copy.start()

    def complete(group):
        for copy in group["near"] + group["back"] + group["last"]:
            copy.wait()
        for copy in group["far"] + group["side"]:
            copy.wait_send()

    def over_feat(make):
        base = sems(feats)
        return [make(k, base + k, feat_at(k)) for k in range(1, feats)]

    each(lambda k: node_copy(0, k).start())
    def wide_cols(who):
        return wide.at[0, :, at(who, share)]

    wide_near = remote(nodes, wide_cols(f), sems(1), feat=partner)
    wide_far = [remote(nodes, wide_cols(f), sems(1), feat=chip_at(m)) for m in chips]
    wide_back = [remote(wide_cols(chip_from(m)), wide_cols(chip_from(m)), sems(1), feat=partner) for m in chips]
    for copy in wide_far + [wide_near]:
        copy.start()
    begin(weights_in[0])
    begin(weights_out[0])
    small = []
    for src, dst in ((nbias, nb), (ngain, ng), (nshift, ns)):
        small += over_feat(lambda k, sem, who, src=src, dst=dst: remote(src, dst.at[f], sem, feat=who))
    cell_copies = over_feat(
        lambda k, sem, dst: remote(grid_hbm.at[at(dst, cell_count), :], cells.at[:, at(f, share)], sem, feat=dst)
    )
    for copy in small + cell_copies:
        copy.start()

    fill_picks(pick_slot, slot_row[...])
    fill_picks(pick_recv, recv_row[...])
    node_id = lax.broadcasted_iota(jnp.int32, sum_recv.shape, 0)
    sum_recv[...] = jnp.where(node_id == recv_row[...], 1.0, 0.0).astype(BF16)
    fill_picks(pick_link, link_row[...])
    fill_picks(pick_link_table, link_table_row[...])
    link_id = lax.broadcasted_iota(jnp.int32, pick_cell.shape, 0)
    cell_id = 3 * lax.broadcasted_iota(jnp.int32, pick_cell.shape, 1)
    pick_cell[...] = jnp.where((link_id >= cell_id) & (link_id < cell_id + 3), 1.0, 0.0).astype(BF16)
    link_id = lax.broadcasted_iota(jnp.int32, sum_cell.shape, 1)
    cell_id = 3 * lax.broadcasted_iota(jnp.int32, sum_cell.shape, 0)
    sum_cell[...] = jnp.where((link_id >= cell_id) & (link_id < cell_id + 3), 1.0, 0.0).astype(BF16)

    def tiles(count, fn):
        tile = count // 2

        def body(i, carry):
            fn(at(i, tile))
            return carry

        lax.fori_loop(0, 2, body, 0)

    def edge_start(t, state):
        loads[("ew_in", t)].wait()
        loads[("ew_out", t)].wait()

        def body(rows):
            acc[rows, :] = dot(state[rows, :], ew_in[t, 0]) + ebias[t, 0:1, :]

        tiles(state.shape[0], body)

    def edge_receivers(t, state, picks, source):
        def body(rows):
            got = dot(picks[rows, :], source[...]).astype(BF16)
            acc[rows, :] += dot(got, ew_in[t, 2])

        tiles(state.shape[0], body)

    def edge_finish(t, state, picks):
        def body(rows):
            got = dot(picks[rows, :], arrived[t, : counts[t], :]).astype(BF16)
            pre = acc[rows, :] + dot(got, ew_in[t, 1])
            state[rows, :] = finish_mlp(
                pre, state[rows, :], ew_out[t], ebias[t, 1:2, :], egain[t : t + 1, :], eshift[t : t + 1, :]
            )

        tiles(state.shape[0], body)

    def node_mlp(t, latent, summed):
        def row(ref, *index):
            return jnp.concatenate([ref[(g, t) + index] for g in range(feats)], axis=-1).reshape(1, -1)

        pre = dot(latent, nw_in[t, 0]) + dot(summed, nw_in[t, 1]) + row(nb, 0)
        return finish_mlp(pre, latent, nw_out[t], row(nb, 1), row(ng), row(ns))

    mine = at(core, own_rows)
    for t in range(sections):
        state = links if t == last else edges
        if t == 0:
            loads["edges"].wait()
        else:
            outgoing[t, : counts[t], :] = dot(pick_refs[t][...], wide[t, :, at(f, share)]).astype(BF16)
            send = lambda k, t=t: node_copy(t, k).start()
            each(lambda k: if_close(node_at(k), None, lambda: send(k)))
            each(lambda k: if_close(node_at(k), lambda: send(k), None))
            for m in chips:
                cols = wide[t, :, at(chip_from(m), share)]
                extra[t, m, : counts[t], :] = dot(pick_refs[t][...], cols).astype(BF16)
            each(lambda k, t=t: extra_start(t, k))
            if t == last:
                loads["links"].wait()
        edge_start(t, state)
        if t == 0:
            loads["wide"].wait()
            for copy, back in zip(wide_far, wide_back):
                copy.wait_recv()
                back.start()
            for copy in [wide_near] + wide_back:
                copy.wait()
            for copy in wide_far:
                copy.wait_send()
        own_slots = at(p, slots[t])
        arrived[t, own_slots, :] = dot(pick_refs[t][own_slots, :], wide[t]).astype(BF16)
        if t == last:
            loads["cells"].wait()
            for copy in cell_copies:
                copy.wait()
            edge_receivers(t, state, pick_cell, cells)
        else:
            edge_receivers(t, state, pick_recv, wide.at[t])
        spread(t)
        pass_on(weights_in[t])
        pass_on(weights_out[t])
        settle(t)
        edge_finish(t, state, pick_link if t == last else pick_slot)
        if t < last:
            part[t] = dot(sum_recv[at(1 - core, own_rows), :], edges[...]).astype(BF16)
            pair = remote(part.at[t], rs_buf.at[t, 0], sems(1), feat=partner)
            pair.start()
            total = dot(sum_recv[mine, :], edges[...])
            pair.wait()
            chip_sum[t] = (total + rs_buf[t, 0].astype(F32)).astype(BF16)
            sum_copies = [remote(chip_sum.at[t], rs_buf.at[t, m], sems(1), feat=chip_at(m)) for m in chips]
            for copy in sum_copies:
                copy.start()
        pass_last(weights_in[t])
        pass_last(weights_out[t])
        if t < last:
            begin(weights_in[t + 1])
            begin(weights_out[t + 1])
        if t == 0:
            for name in ("nb", "ng", "ns"):
                loads[name].wait()
            for copy in small:
                copy.wait()
        loads[("nw_in", t)].wait()
        loads[("nw_out", t)].wait()
        complete(weights_in[t])
        complete(weights_out[t])
        if t < last:
            summed = chip_sum[t].astype(F32)
            for m, copy in zip(chips, sum_copies):
                copy.wait()
                summed += rs_buf[t, m].astype(F32)
            wide[t + 1, mine, :] = node_mlp(t, wide[t, mine, :], summed.astype(BF16))
            row_copy = remote(wide.at[t + 1, mine, :], wide.at[t + 1, mine, :], sems(1), feat=partner)
            row_copy.start()
            row_copy.wait()
    gathered = dot(sum_cell[...], links[...]).astype(BF16)
    upd[...] = node_mlp(last, cells[...], gathered)
    out_copies = over_feat(
        lambda k, sem, dst: remote(upd.at[:, at(dst, share)], out.at[at(f, cell_count), :], sem, feat=dst)
    )
    for copy in out_copies:
        copy.start()
    out[at(f, cell_count), :] = upd[:, at(f, share)]
    for copy in out_copies:
        copy.wait()
    assert next_sem[0] <= send_sem.shape[0]


def solution(mesh):
    n, feats = mesh.shape["node"], mesh.shape["feat"]

    def local(
        mesh_nodes, mesh_edges, grid_nodes, m2g_edges, edge_receivers, edge_slots, send_rows, m2g_slots,
        m2g_send_rows, edge_w_in, edge_w_out, edge_bias, edge_gain, edge_shift, node_w_in, node_w_out,
        node_bias, node_gain, node_shift,
    ):
        rows, share = mesh_nodes.shape
        edge_count, width = mesh_edges.shape
        link_count = m2g_edges.shape[0]
        sections = edge_w_in.shape[0]
        buf, link_buf = send_rows.size, m2g_send_rows.size
        cell_count = grid_nodes.shape[0] // feats
        counts = (buf,) * (sections - 1) + (link_buf,)
        top = max(counts)
        half = feats // 2
        sem_count = sections * n * (2 + 3 * (half - 1)) + 2 * sections * (1 + 4 * half) + feats * 6 + sections * feats + 2 * half
        vmem = pl.BlockSpec(memory_space=pltpu.VMEM)
        hbm = pl.BlockSpec(memory_space=pl.ANY)

        def v(*shape, dtype=BF16):
            return pltpu.VMEM(shape, dtype)

        return pl.pallas_call(
            functools.partial(kernel, n, feats, counts),
            name="graph_layers",
            out_shape=jax.ShapeDtypeStruct(grid_nodes.shape, BF16),
            in_specs=[
                vmem, hbm, hbm, hbm, vmem, vmem, vmem, vmem, vmem,
                hbm, hbm, vmem, vmem, vmem, hbm, hbm, vmem, vmem, vmem,
            ],
            out_specs=vmem,
            scratch_shapes=[
                v(edge_count, width), v(link_count, width),
                v(*edge_w_in.shape), v(*edge_w_out.shape),
                v(sections, 2, width, width), v(sections, width, width),
                v(feats, *node_bias.shape, dtype=F32), v(feats, *node_gain.shape, dtype=F32),
                v(feats, *node_shift.shape, dtype=F32),
                v(buf, rows), v(link_buf, rows), v(edge_count, buf), v(edge_count, rows), v(rows, edge_count),
                v(link_count, link_buf), v(link_count, cell_count), v(cell_count, link_count),
                v(max(edge_count, link_count), width, dtype=F32),
                v(sections - 1, rows // 2, width), v(sections - 1, rows // 2, width),
                v(sections - 1, half, rows // 2, width),
                v(cell_count, width), v(cell_count, width),
                v(sections, rows, width), v(sections, top, share), v(sections, half, top, share),
                v(sections, top, width),
                pltpu.SemaphoreType.DMA((7 + 4 * sections,)),
                pltpu.SemaphoreType.DMA((sem_count,)),
                pltpu.SemaphoreType.DMA((sem_count,)),
            ],
            compiler_params=pltpu.CompilerParams(
                collective_id=0, has_side_effects=True, vmem_limit_bytes=56 * 1024 * 1024
            ),
        )(
            mesh_nodes, mesh_edges, grid_nodes, m2g_edges, edge_receivers.reshape(1, -1), edge_slots.reshape(1, -1),
            send_rows.reshape(1, -1), m2g_slots.reshape(1, -1), m2g_send_rows.reshape(1, -1),
            edge_w_in, edge_w_out, edge_bias, edge_gain, edge_shift, node_w_in, node_w_out,
            node_bias, node_gain, node_shift,
        )

    in_specs = (
        P("node", "feat"), P(("node", "feat"), None), P("node", "feat"), P(("node", "feat"), None),
        P(("node", "feat")), P(("node", "feat")), P("node", None, None), P(("node", "feat")),
        P("node", None, None), P(), P(), P(), P(), P(), P(None, None, "feat", None),
        P(None, "feat", None), P(None, None, "feat"), P(None, "feat"), P(None, "feat"),
    )
    return jax.shard_map(local, mesh=mesh, in_specs=in_specs, out_specs=P("node", "feat"), check_vma=False)
```

profile of v0, /device:TPU:0, one launch (start us, length us, event | category | flops | bytes accessed | tf_op | source)
XLA Modules:
  0.0 85.6 jit_solution(3386906612261944903)
XLA Ops:
  0.0 1.2 %reshape.18.refs_7_ = s32[1,384]{1,0:T(1,128)} reshape(s32[384]{0:T(512)} %param.26) | data formatting | bytes 3072 | tf_op jit(solution)/shard_map/reshape | solution.py:535
  1.2 82.7 %graph_layers.1 = bf16[512,128]{1,0:T(8,128)(2,1)} custom-call(bf16[256,128]{1,0:T(8,128)(2,1)} %refs_0_.1, bf16[512,512]{1,0:T(8,128)(2,1)} %refs_1_.1, bf16[512,128]{1,0:T(8,128)(2,1)} %refs_2_.1, bf16[384,512]{1,0:T(8,128)(2,1)} %refs_3_.1, s32[1,512]{1,0:T(1,128)} %bitcast.6, s32[1,512]{1,0:T(1,128)} %bitcast.7, s32[1,1024]{1,0:T(1,128)} %bitcast.4, ...), custom_call_target="tpu_custom_call" | custom-call | tf_op jit(solution)/shard_map/graph_layers/pallas_call | solution.py:503
  84.0 1.6 %copy.21 = bf16[512,128]{1,0:T(8,128)(2,1)} copy(bf16[512,128]{1,0:T(8,128)(2,1)} %graph_layers.1) | data formatting | bytes 262144
where the time goes:
time: 85.8 us; the launch traced here: 85.6 us
  Pallas kernels  82.7 us (96%)
  local copies, waits for them, and re-layouts  2.81 us (3%)
    pallas_call x1, Pallas kernels, local(): pl.pallas_call(functools.partial(kernel, n, feats, counts), name='graph_l...  82.7 us

commit v1 on v0

--- a/solution.py
+++ b/solution.py
@@ -34,7 +34,8 @@
 
 
 def finish_mlp(pre, base, w_out, bias_out, gain, shift):
-    hidden = (pre / (1.0 + jnp.exp(-pre))).astype(BF16)
+    h = 0.5 * pre
+    hidden = (h + h * jnp.tanh(h)).astype(BF16)
     out = dot(hidden, w_out) + bias_out
     mean = jnp.mean(out, axis=-1, keepdims=True)
     variance = jnp.mean(out * out, axis=-1, keepdims=True) - mean * mean
@@ -49,7 +50,7 @@
         out,
         edges, links, ew_in, ew_out, nw_in, nw_out, nb, ng, ns,
         pick_table, pick_link_table, pick_slot, pick_recv, sum_recv, pick_link, pick_cell, sum_cell,
-        acc, part, chip_sum, rs_buf, cells, upd, wide, outgoing, extra, arrived,
+        acc, part, chip_sum, rs_buf, cells, upd, wide, outgoing, extra, arrived, latent_pre,
         load_sem, send_sem, recv_sem,
     ) = refs
     sections = ew_in.shape[0]
@@ -79,11 +80,17 @@
             device_id=where, device_id_type=MESH,
         )
 
-    def node_at(k):
-        return lax.rem(p + k, n)
-
-    def node_from(k):
-        return lax.rem(p + n - k, n)
+    def peer(k):
+        out, bit = p, 1
+        while bit < n:
+            if isinstance(k, int):
+                if k & bit:
+                    out = out + bit * (1 - 2 * lax.rem(lax.div(p, bit), 2))
+            else:
+                ours, theirs = lax.rem(lax.div(p, bit), 2), lax.rem(lax.div(k, bit), 2)
+                out = out + bit * (lax.rem(ours + theirs, 2) - ours)
+            bit *= 2
+        return out
 
     def feat_at(k):
         return lax.rem(f + k, feats)
@@ -97,7 +104,7 @@
     barrier = pltpu.get_barrier_semaphore()
 
     def greet(k, carry):
-        pl.semaphore_signal(barrier, inc=1, device_id={"node": node_at(k)}, device_id_type=MESH)
+        pl.semaphore_signal(barrier, inc=1, device_id={"node": peer(k)}, device_id_type=MESH)
         return carry
 
     lax.fori_loop(1, n, greet, 0)
@@ -126,6 +133,7 @@
 
     pick_refs = [pick_table] * last + [pick_link_table]
     slots = [c // n for c in counts]
+    groups = [min(2 * LANES // s, n // 2) for s in slots]
 
     fill_picks(pick_table, table_row[...])
     first_out = dot(pick_table[...], nodes[...]).astype(BF16)
@@ -136,126 +144,96 @@
     node_sem = [sems(n) for _ in range(sections)]
     near_sem = [sems(n) for _ in range(sections)]
     chips = range(1, half)
-    far_sem = [{m: sems(n) for m in chips} for _ in range(sections)]
+    swap_sem = [{m: sems(n) for m in chips} for _ in range(sections)]
     relay_sem = [{m: sems(n) for m in chips} for _ in range(sections)]
-    extra_sem = [{m: sems(n) for m in chips} for _ in range(sections)]
+
+    def each(fn, ks):
+        if len(ks) <= 8:
+            for k in ks:
+                fn(k)
+        else:
+
+            def body(i, carry):
+                fn(ks.start + i * ks.step)
+                return carry
+
+            lax.fori_loop(0, len(ks), body, 0)
+
+    far = range(n - 1, n // 2 - 1, -1)
+    close = range(1, n // 2)
 
     def node_copy(t, k):
-        dst = node_at(k)
+        dst = peer(k)
         return remote(
             outgoing.at[t, at(dst, slots[t]), :],
             arrived.at[t, at(p, slots[t]), at(f, share)],
             node_sem[t] + k, node=dst,
         )
 
+    def block(t, k, who):
+        return arrived.at[t, at(peer(k), slots[t]), at(who, share)]
+
+    def near_copy(t, k):
+        return remote(block(t, k, f), block(t, k, f), near_sem[t] + k, feat=partner)
+
+    def far_copy(t, k, m):
+        return remote(block(t, k, f), block(t, k, f), swap_sem[t][m] + k, feat=chip_at(m))
+
     def extra_copy(t, k, m):
-        dst = node_at(k)
+        dst = peer(k)
         return remote(
             extra.at[t, m, at(dst, slots[t]), :],
             arrived.at[t, at(p, slots[t]), at(chip_from(m), share)],
-            extra_sem[t][m] + k, node=dst,
+            swap_sem[t][m] + k, node=dst,
         )
-
-    def if_close(other, yes, no):
-        close = lax.div(other, block_half) == lax.div(p, block_half)
-        if yes is not None:
-            pl.when(close)(yes)
-        if no is not None:
-            pl.when(jnp.logical_not(close))(no)
-
-    def block(t, k, who):
-        return arrived.at[t, at(node_from(k), slots[t]), at(who, share)]
-
-    def near_copy(t, k):
-        return remote(block(t, k, f), block(t, k, f), near_sem[t] + k, feat=partner)
-
-    def far_copy(t, k, m):
-        return remote(block(t, k, f), block(t, k, f), far_sem[t][m] + k, feat=chip_at(m))
 
     def relay_copy(t, k, m):
         who = chip_from(m)
         return remote(block(t, k, who), block(t, k, who), relay_sem[t][m] + k, feat=partner)
 
-    def each(fn, low=1, high=n):
-        def body(k, carry):
-            fn(k)
-            return carry
-
-        lax.fori_loop(low, high, body, 0)
-
-    def spread(t):
-        lag = 2
-
-        def relay_now(k):
+    def take_far(t, k):
+        node_copy(t, k).wait_recv()
+        for m in chips:
+            far_copy(t, k, m).start()
+        near_copy(t, k).start()
+
+    def take_close(t, k):
+        node_copy(t, k).wait_recv()
+        near_copy(t, k).start()
+
+    def relay_far(t, k):
+        for m in chips:
+            far_copy(t, k, m).wait_recv()
+            relay_copy(t, k, m).start()
+
+    def relay_close(t, k):
+        for m in chips:
+            extra_copy(t, k, m).wait_recv()
+            relay_copy(t, k, m).start()
+
+    def arrive(t, k):
+        near_copy(t, k).wait_recv()
+        for m in chips:
+            relay_copy(t, k, m).wait_recv()
+
+    def settle(t):
+        def sent(k):
+            node_copy(t, k).wait_send()
+            near_copy(t, k).wait_send()
             for m in chips:
-                far_copy(t, k, m).wait_recv()
-                relay_copy(t, k, m).start()
-
-        def far_start(k):
-            for m in chips:
-                far_copy(t, k, m).start()
-
-        def extra_relay(k):
-            for m in chips:
-                extra_copy(t, k, m).wait_recv()
-                relay_copy(t, k, m).start()
-
-        def take(k):
-            node_copy(t, k).wait_recv()
-            near_copy(t, k).start()
-
-        def step(k):
-            take(k)
-            far_start(k)
-
-            @pl.when(k > lag)
-            def _():
-                relay_now(k - lag)
-
-        def cross(k):
-            take(k)
-            far_start(k)
-
-        def direct(k):
-            take(k)
-            extra_relay(k)
-
-        if t == 0:
-            each(step)
-            each(relay_now, max(1, n - lag), n)
-        else:
-            each(lambda k: if_close(node_from(k), None, lambda: cross(k)))
-            each(lambda k: if_close(node_from(k), lambda: direct(k), None))
-            each(lambda k: if_close(node_from(k), None, lambda: relay_now(k)))
-
-    def settle(t):
-        def far_done(k):
+                relay_copy(t, k, m).wait_send()
+
+        def far_sent(k):
             for m in chips:
                 far_copy(t, k, m).wait_send()
 
-        def extra_done(k):
+        def close_sent(k):
             for m in chips:
                 extra_copy(t, k, m).wait_send()
 
-        def step(k):
-            node_copy(t, k).wait_send()
-            near_copy(t, k).wait()
-            if t == 0:
-                far_done(k)
-            else:
-                if_close(node_from(k), None, lambda: far_done(k))
-                if_close(node_at(k), lambda: extra_done(k), None)
-            for m in chips:
-                relay_copy(t, k, m).wait()
-
-        each(step)
-
-    def extra_start(t, k):
-        def go():
-            for m in chips:
-                extra_copy(t, k, m).start()
-
-        if_close(node_at(k), go, None)
+        each(sent, range(1, n))
+        each(far_sent, far)
+        each(close_sent, close)
 
     def weight_copies(near_src, near_dst, half_src, half_dst):
         group = {"near": [remote(near_src, near_dst, sems(1), feat=partner)]}
@@ -315,7 +293,9 @@
         base = sems(feats)
         return [make(k, base + k, feat_at(k)) for k in range(1, feats)]
 
-    each(lambda k: node_copy(0, k).start())
+    each(lambda k: node_copy(0, k).start(), far)
+    each(lambda k: node_copy(0, k).start(), close)
+
     def wide_cols(who):
         return wide.at[0, :, at(who, share)]
 
@@ -332,14 +312,14 @@
     cell_copies = over_feat(
         lambda k, sem, dst: remote(grid_hbm.at[at(dst, cell_count), :], cells.at[:, at(f, share)], sem, feat=dst)
     )
-    for copy in small + cell_copies:
+    for copy in small:
         copy.start()
 
     fill_picks(pick_slot, slot_row[...])
     fill_picks(pick_recv, recv_row[...])
     node_id = lax.broadcasted_iota(jnp.int32, sum_recv.shape, 0)
     sum_recv[...] = jnp.where(node_id == recv_row[...], 1.0, 0.0).astype(BF16)
-    fill_picks(pick_link, link_row[...])
+    fill_picks(pick_link, link_row[...].reshape(1, -1))
     fill_picks(pick_link_table, link_table_row[...])
     link_id = lax.broadcasted_iota(jnp.int32, pick_cell.shape, 0)
     cell_id = 3 * lax.broadcasted_iota(jnp.int32, pick_cell.shape, 1)
@@ -348,88 +328,122 @@
     cell_id = 3 * lax.broadcasted_iota(jnp.int32, sum_cell.shape, 0)
     sum_cell[...] = jnp.where((link_id >= cell_id) & (link_id < cell_id + 3), 1.0, 0.0).astype(BF16)
 
-    def tiles(count, fn):
+    def halves(count):
         tile = count // 2
-
-        def body(i, carry):
-            fn(at(i, tile))
-            return carry
-
-        lax.fori_loop(0, 2, body, 0)
-
-    def edge_start(t, state):
+        return [slice(i * tile, (i + 1) * tile) for i in range(2)]
+
+    def edge_base(t, state, picks, source):
         loads[("ew_in", t)].wait()
         loads[("ew_out", t)].wait()
-
-        def body(rows):
-            acc[rows, :] = dot(state[rows, :], ew_in[t, 0]) + ebias[t, 0:1, :]
-
-        tiles(state.shape[0], body)
-
-    def edge_receivers(t, state, picks, source):
-        def body(rows):
-            got = dot(picks[rows, :], source[...]).astype(BF16)
-            acc[rows, :] += dot(got, ew_in[t, 2])
-
-        tiles(state.shape[0], body)
-
-    def edge_finish(t, state, picks):
-        def body(rows):
-            got = dot(picks[rows, :], arrived[t, : counts[t], :]).astype(BF16)
-            pre = acc[rows, :] + dot(got, ew_in[t, 1])
+        got = dot(source[...], ew_in[t, 2]).astype(BF16)
+        for rows in halves(state.shape[0]):
+            acc[rows, :] = dot(state[rows, :], ew_in[t, 0]) + dot(picks[rows, :], got) + ebias[t, 0:1, :]
+
+    def group_of(t, j):
+        group = groups[t]
+        rows = at(lax.div(peer(j * group), group), group * slots[t])
+        return rows, dot(arrived[t, rows, :], ew_in[t, 1]).astype(BF16)
+
+    def group_ks(t, j):
+        return range(max(1, j * groups[t]), (j + 1) * groups[t])
+
+    def edge_group(t, state, picks, j):
+        each(lambda k: arrive(t, k), group_ks(t, j))
+        cols, got = group_of(t, j)
+        for rows in halves(state.shape[0]):
+            acc[rows, :] += dot(picks[rows, cols], got)
+
+    def edge_finish(t, state, picks, j):
+        each(lambda k: arrive(t, k), group_ks(t, j))
+        cols, got = group_of(t, j)
+        for rows in halves(state.shape[0]):
+            pre = acc[rows, :] + dot(picks[rows, cols], got)
             state[rows, :] = finish_mlp(
                 pre, state[rows, :], ew_out[t], ebias[t, 1:2, :], egain[t : t + 1, :], eshift[t : t + 1, :]
             )
 
-        tiles(state.shape[0], body)
-
-    def node_mlp(t, latent, summed):
-        def row(ref, *index):
-            return jnp.concatenate([ref[(g, t) + index] for g in range(feats)], axis=-1).reshape(1, -1)
-
-        pre = dot(latent, nw_in[t, 0]) + dot(summed, nw_in[t, 1]) + row(nb, 0)
-        return finish_mlp(pre, latent, nw_out[t], row(nb, 1), row(ng), row(ns))
+    def row(ref, t, *index):
+        return jnp.concatenate([ref[(g, t) + index] for g in range(feats)], axis=-1).reshape(1, -1)
+
+    def node_start(t, latent):
+        latent_pre[: latent.shape[0], :] = dot(latent, nw_in[t, 0]) + row(nb, t, 0)
+
+    def node_finish(t, latent, summed):
+        pre = dot(summed, nw_in[t, 1]) + latent_pre[: latent.shape[0], :]
+        return finish_mlp(pre, latent, nw_out[t], row(nb, t, 1), row(ng, t), row(ns, t))
+
+    def weights_done(t):
+        pass_last(weights_in[t])
+        pass_last(weights_out[t])
+
+    def weights_ready(t):
+        loads[("nw_in", t)].wait()
+        loads[("nw_out", t)].wait()
+        complete(weights_in[t])
+        complete(weights_out[t])
 
     mine = at(core, own_rows)
     for t in range(sections):
         state = links if t == last else edges
+        picks = pick_link if t == last else pick_slot
+        count = n // groups[t]
+        far_groups = list(range(count - 1, count // 2 - 1, -1))
         if t == 0:
             loads["edges"].wait()
-        else:
-            outgoing[t, : counts[t], :] = dot(pick_refs[t][...], wide[t, :, at(f, share)]).astype(BF16)
-            send = lambda k, t=t: node_copy(t, k).start()
-            each(lambda k: if_close(node_at(k), None, lambda: send(k)))
-            each(lambda k: if_close(node_at(k), lambda: send(k), None))
-            for m in chips:
-                cols = wide[t, :, at(chip_from(m), share)]
-                extra[t, m, : counts[t], :] = dot(pick_refs[t][...], cols).astype(BF16)
-            each(lambda k, t=t: extra_start(t, k))
-            if t == last:
-                loads["links"].wait()
-        edge_start(t, state)
-        if t == 0:
             loads["wide"].wait()
             for copy, back in zip(wide_far, wide_back):
                 copy.wait_recv()
                 back.start()
             for copy in [wide_near] + wide_back:
-                copy.wait()
-            for copy in wide_far:
-                copy.wait_send()
+                copy.wait_recv()
+        else:
+            outgoing[t, : counts[t], :] = dot(pick_refs[t][...], wide[t, :, at(f, share)]).astype(BF16)
+            each(lambda k, t=t: node_copy(t, k).start(), far)
+            each(lambda k, t=t: node_copy(t, k).start(), close)
+            if t == last:
+                loads["links"].wait()
+        for m in chips:
+            cols = wide[t, :, at(chip_from(m), share)]
+            extra[t, m, : counts[t], :] = dot(pick_refs[t][...], cols).astype(BF16)
+
+        def extra_start(k, t=t):
+            for m in chips:
+                extra_copy(t, k, m).start()
+
+        each(extra_start, close)
         own_slots = at(p, slots[t])
         arrived[t, own_slots, :] = dot(pick_refs[t][own_slots, :], wide[t]).astype(BF16)
         if t == last:
             loads["cells"].wait()
             for copy in cell_copies:
                 copy.wait()
-            edge_receivers(t, state, pick_cell, cells)
+            edge_base(t, state, pick_cell, cells)
         else:
-            edge_receivers(t, state, pick_recv, wide.at[t])
-        spread(t)
-        pass_on(weights_in[t])
-        pass_on(weights_out[t])
-        settle(t)
-        edge_finish(t, state, pick_link if t == last else pick_slot)
+            edge_base(t, state, pick_recv, wide.at[t])
+        for i, j in enumerate(far_groups):
+            each(lambda k, t=t: take_far(t, k), group_ks(t, j)[::-1])
+            if i == 0:
+                if t > 0:
+                    pass_on(weights_in[t])
+                    pass_on(weights_out[t])
+                each(lambda k, t=t: take_close(t, k), close)
+                each(lambda k, t=t: relay_close(t, k), close)
+        if t == 0:
+            pass_on(weights_in[t])
+            pass_on(weights_out[t])
+        for i, j in enumerate(far_groups):
+            if t > 0 and i == len(far_groups) - 1:
+                weights_done(t)
+            each(lambda k, t=t: relay_far(t, k), group_ks(t, j)[::-1])
+            if i == 0:
+                for c in range(count // 2):
+                    edge_group(t, state, picks, c)
+            else:
+                edge_group(t, state, picks, far_groups[i - 1])
+        if t == last:
+            weights_ready(t)
+            node_start(t, cells[...])
+        edge_finish(t, state, picks, far_groups[-1])
         if t < last:
             part[t] = dot(sum_recv[at(1 - core, own_rows), :], edges[...]).astype(BF16)
             pair = remote(part.at[t], rs_buf.at[t, 0], sems(1), feat=partner)
@@ -440,37 +454,38 @@
             sum_copies = [remote(chip_sum.at[t], rs_buf.at[t, m], sems(1), feat=chip_at(m)) for m in chips]
             for copy in sum_copies:
                 copy.start()
-        pass_last(weights_in[t])
-        pass_last(weights_out[t])
-        if t < last:
-            begin(weights_in[t + 1])
-            begin(weights_out[t + 1])
-        if t == 0:
-            for name in ("nb", "ng", "ns"):
-                loads[name].wait()
-            for copy in small:
-                copy.wait()
-        loads[("nw_in", t)].wait()
-        loads[("nw_out", t)].wait()
-        complete(weights_in[t])
-        complete(weights_out[t])
-        if t < last:
+            if t == 0:
+                for copy in cell_copies:
+                    copy.start()
+                weights_done(t)
+                for copy in [wide_near] + wide_far + wide_back:
+                    copy.wait_send()
+                for name in ("nb", "ng", "ns"):
+                    loads[name].wait()
+                for copy in small:
+                    copy.wait()
+            settle(t)
+            weights_ready(t)
+            node_start(t, wide[t, mine, :])
             summed = chip_sum[t].astype(F32)
             for m, copy in zip(chips, sum_copies):
                 copy.wait()
                 summed += rs_buf[t, m].astype(F32)
-            wide[t + 1, mine, :] = node_mlp(t, wide[t, mine, :], summed.astype(BF16))
+            begin(weights_in[t + 1])
+            begin(weights_out[t + 1])
+            wide[t + 1, mine, :] = node_finish(t, wide[t, mine, :], summed.astype(BF16))
             row_copy = remote(wide.at[t + 1, mine, :], wide.at[t + 1, mine, :], sems(1), feat=partner)
             row_copy.start()
             row_copy.wait()
     gathered = dot(sum_cell[...], links[...]).astype(BF16)
-    upd[...] = node_mlp(last, cells[...], gathered)
+    upd[...] = node_finish(last, cells[...], gathered)
     out_copies = over_feat(
         lambda k, sem, dst: remote(upd.at[:, at(dst, share)], out.at[at(f, cell_count), :], sem, feat=dst)
     )
     for copy in out_copies:
         copy.start()
     out[at(f, cell_count), :] = upd[:, at(f, share)]
+    settle(last)
     for copy in out_copies:
         copy.wait()
     assert next_sem[0] <= send_sem.shape[0]
@@ -522,7 +537,7 @@
                 v(sections - 1, half, rows // 2, width),
                 v(cell_count, width), v(cell_count, width),
                 v(sections, rows, width), v(sections, top, share), v(sections, half, top, share),
-                v(sections, top, width),
+                v(sections, top, width), v(max(rows // 2, cell_count), width, dtype=F32),
                 pltpu.SemaphoreType.DMA((7 + 4 * sections,)),
                 pltpu.SemaphoreType.DMA((sem_count,)),
                 pltpu.SemaphoreType.DMA((sem_count,)),
@@ -532,7 +547,7 @@
             ),
         )(
             mesh_nodes, mesh_edges, grid_nodes, m2g_edges, edge_receivers.reshape(1, -1), edge_slots.reshape(1, -1),
-            send_rows.reshape(1, -1), m2g_slots.reshape(1, -1), m2g_send_rows.reshape(1, -1),
+            send_rows.reshape(1, -1), m2g_slots, m2g_send_rows.reshape(1, -1),
             edge_w_in, edge_w_out, edge_bias, edge_gain, edge_shift, node_w_in, node_w_out,
             node_bias, node_gain, node_shift,
         )

time: 85.8 us -> 76.7 us (0.89)
  Pallas kernels: 82.7 us -> 75 us
  local copies, waits for them, and re-layouts: 2.81 us -> 1.57 us
    pallas_call x1, Pallas kernels: 82.7 us -> 75 us  [local(): pl.pallas_call(functools.partial(kernel, n, feats, counts), name='graph_l...]
    reshape x1 -> x0, local copies, waits for them, and re-layouts: 1.24 us -> none  [local(): m2g_slots.reshape(1, -1)]
where the time goes in v1:
time: 76.7 us; the launch traced here: 76.5 us
  Pallas kernels  75 us (98%)
  local copies, waits for them, and re-layouts  1.57 us (2%)
    pallas_call x1, Pallas kernels, local(): pl.pallas_call(functools.partial(kernel, n, feats, counts), name='graph_l...  75 us
    unnamed x1, local copies, waits for them, and re-layouts  1.57 us

profile of v1, /device:TPU:0, one launch (start us, length us, event | category | flops | bytes accessed | tf_op | source)
XLA Modules:
  0.0 76.5 jit_solution(797836187967504977)
XLA Ops:
  0.0 75.0 %graph_layers.1 = bf16[512,128]{1,0:T(8,128)(2,1)} custom-call(bf16[256,128]{1,0:T(8,128)(2,1)} %refs_0_.1, bf16[512,512]{1,0:T(8,128)(2,1)} %refs_1_.1, bf16[512,128]{1,0:T(8,128)(2,1)} %refs_2_.1, bf16[384,512]{1,0:T(8,128)(2,1)} %refs_3_.1, s32[1,512]{1,0:T(1,128)} %bitcast.6, s32[1,512]{1,0:T(1,128)} %bitcast.7, s32[1,1024]{1,0:T(1,128)} %bitcast.4, ...), custom_call_target="tpu_custom_call" | custom-call | tf_op jit(solution)/shard_map/graph_layers/pallas_call | solution.py:518
  75.0 1.6 %copy.21 = bf16[512,128]{1,0:T(8,128)(2,1)} copy(bf16[512,128]{1,0:T(8,128)(2,1)} %graph_layers.1) | data formatting | bytes 262144
